TPU v7x, 32 devices: a whole 2x2x4 slice. The times are simulated.
32 devices in a mesh: dp: 2 (over x), tp: 4 (over z), cp: 4 (over y, core).
Axes of the slice: x: 2, y: 2, z: 4, core: 2. Of those that a mesh axis runs over, the one named last changes fastest.
Arguments:
- hidden: bfloat16 [4096, 2048], P(('dp', 'cp')), parts along dimension 0
- seg_ids: int32 [4096], P(('dp', 'cp')), parts along dimension 0
- w_q: bfloat16 [2048, 2048], P(None, 'tp')
- b_q: bfloat16 [2048], P('tp')
- w_kv: bfloat16 [2048, 256], replicated
- b_kv: bfloat16 [256], replicated
- w_o: bfloat16 [2048, 2048], P('tp')
- b_o: bfloat16 [2048], replicated
- ln_gain: bfloat16 [2048], replicated
- ln_bias: bfloat16 [2048], replicated
Outputs:
- output 1: bfloat16 [4096, 2048], P(('dp', 'cp')), parts along dimension 0
- output 2: bfloat16 [4096, 128], P(('dp', 'cp')), parts along dimension 0
- output 3: bfloat16 [4096, 128], P(('dp', 'cp')), parts along dimension 0
There are 2 independent parts. A program takes and returns all parts, laid end to end along the dimension named above; an argument that names none is the same for every part.
All inputs are finite; a program needn't handle non-finite values.
Results may differ from a plain program's by a relative error of at most 0.0128857.
Values are sent between devices in bfloat16 or wider.
A program may use at most 1 GiB of HBM per device.

v0:
```python
import functools
import jax
import jax.numpy as jnp
from jax import lax
from jax.experimental import pallas as pl
from jax.experimental.pallas import tpu as pltpu
from jax.sharding import PartitionSpec as P

HEAD_DIM = 128
LN_EPS = 1e-5
SCORE_SCALE = HEAD_DIM ** -0.5 * 1.4426950408889634
MESH = pl.DeviceIdType.MESH
BF16 = jnp.bfloat16
F32 = jnp.float32


def send(src, dst, sent, recv, to):
    pltpu.make_async_remote_copy(src_ref=src, dst_ref=dst, send_sem=sent, recv_sem=recv, device_id=to, device_id_type=MESH).start()


def scoped(fn):
    def run(*about):
        with jax.named_scope(fn.__name__ + '_'.join(str(a) for a in about if isinstance(a, (str, int)))):
            return fn(*about)
    return run


def arrived(dst, recv):
    pltpu.make_async_copy(dst, dst, recv).wait()


def kernel(hid_hbm, seg_hbm, wq_hbm, bq_hbm, wkv_hbm, bkv_hbm, wo_hbm, bo_hbm, gain_hbm, lnb_hbm,
           y_ref, k_ref, v_ref,
           hid, normed, wkv, wq, wo, bq_own, bq_pair, bkv_ref, bo_ref, gain_ref, lnb_ref, seg, segcol, kv, q_s, o_all, part, run_s, m_s, l_s, acc_s,
           load_sem, spread_sem, line_sem, kv_sem, small_sem, bq_recv, seg_recv, kv_recv, wq_recv, wo_recv, o_recv):
    tok, d_model = hid.shape
    width = wq.shape[2]
    heads = width // HEAD_DIM
    tile = tok // 4
    q_rows, o_rows = d_model // 8, width // 8
    dp, z, cp = lax.axis_index('dp'), lax.axis_index('tp'), lax.axis_index('cp')
    y, c = cp // 2, cp % 2
    pair = z + 1 - 2 * (z % 2)
    below, above = {'tp': z - 1}, {'tp': z + 1}
    to_x, to_y, to_core = {'dp': 1 - dp}, {'cp': cp + 2 - 4 * y}, {'cp': cp + 1 - 2 * c}
    pos = lambda px, py, pc: px * 4 + py * 2 + pc
    p_me, p_x, p_y, p_d = pos(dp, y, c), pos(1 - dp, y, c), pos(dp, 1 - y, c), pos(1 - dp, 1 - y, c)
    g_a = 1 + z % 2
    g_c = 3 - 3 * (z // 2)
    g_b = 6 - z - g_a - g_c

    loads = [pltpu.make_async_copy(hid_hbm, hid, load_sem.at[0]),
             pltpu.make_async_copy(wkv_hbm, wkv, load_sem.at[1]),
             pltpu.make_async_copy(wq_hbm, wq.at[0], load_sem.at[2]),
             pltpu.make_async_copy(bq_hbm, bq_own, load_sem.at[3]),
             pltpu.make_async_copy(seg_hbm, seg.at[cp], load_sem.at[4]),
             pltpu.make_async_copy(wo_hbm, wo.at[pl.ds(z * width, width), :], load_sem.at[5]),
             pltpu.make_async_copy(gain_hbm, gain_ref, load_sem.at[6]),
             pltpu.make_async_copy(lnb_hbm, lnb_ref, load_sem.at[7]),
             pltpu.make_async_copy(bkv_hbm, bkv_ref, load_sem.at[8]),
             pltpu.make_async_copy(bo_hbm, bo_ref, load_sem.at[9])]
    for i in (0, 6, 7, 8, 3, 4, 9):
        loads[i].start()

    barrier = pltpu.get_barrier_semaphore()
    for step in (1, 2, 3):
        pl.semaphore_signal(barrier, inc=1, device_id={'cp': (cp + step) % 4}, device_id_type=MESH)
    pl.semaphore_signal(barrier, inc=1, device_id=to_x, device_id_type=MESH)

    @pl.when(z > 0)
    def _():
        pl.semaphore_signal(barrier, inc=1, device_id={'tp': z - 1}, device_id_type=MESH)

    @pl.when(z < 3)
    def _():
        pl.semaphore_signal(barrier, inc=1, device_id={'tp': z + 1}, device_id_type=MESH)

    loads[1].start()
    with jax.named_scope('barr'):
        pl.semaphore_wait(barrier, 5 + (z + 1) // 2 - 2 * (z // 3))

    loads[2].start()
    def q_piece(p, h):
        half = q_rows // 2
        return wq.at[1, pl.ds(pl.multiple_of(p * q_rows + h * half, half), half), :]

    def o_piece(g, p, h):
        half = o_rows // 2
        return wo.at[pl.ds(pl.multiple_of(g * width + p * o_rows + h * half, half), half), :]

    def sem(g, kind, h):
        at = {'z': 0, 'x': 2, 'y': 4, 'd': 6, 'core': 8}[kind] + (0 if kind == 'core' else h)
        return wq_recv.at[at] if g is None else wo_recv.at[g, at]

    middle, edge = (z > 0) & (z < 3), (z == 0) | (z == 3)

    send(bq_hbm, bq_pair, small_sem.at[0], bq_recv, {'tp': pair})
    for h in (0, 1):
        half = q_rows // 2
        send(wq_hbm.at[pl.ds(pl.multiple_of(p_me * q_rows + h * half, half), half), :], q_piece(p_me, h), spread_sem, sem(None, 'z', h),
             {'tp': pair})
    for h in (0, 1):
        half = o_rows // 2
        for to, cond in ((below, z > 0), (above, z < 3)):
            @pl.when(cond)
            def _():
                send(wo_hbm.at[pl.ds(pl.multiple_of(p_me * o_rows + h * half, half), half), :], o_piece(z, p_me, h), line_sem,
                     sem(z, 'z', h), to)
    for step in (1, 2, 3):
        pl.when(cp + step < 4)(lambda: send(seg_hbm, seg.at[cp], small_sem.at[step], seg_recv.at[cp], {'cp': cp + step}))

    def pass_on(g, source, h, by_x):
        p = {'z': p_me, 's': p_me, 'x': p_x, 'y': p_y, 'd': p_d}[source]
        piece = q_piece(p, h) if g is None else o_piece(g, p, h)
        if source == 's':
            send(piece, piece, spread_sem, sem(g, 'x', h), to_x)
            send(piece, piece, spread_sem, sem(g, 'y', h), to_y)
            return
        arrived(piece, sem(g, source, h))
        if source == 'z' and g is not None:
            pl.when((g > z) & (z > 0))(lambda: send(piece, piece, line_sem, sem(g, 'z', h), below))
            pl.when((g < z) & (z < 3))(lambda: send(piece, piece, line_sem, sem(g, 'z', h), above))
        elif source == 'x':
            if not by_x:
                pl.when(c == 1)(lambda: send(piece, piece, spread_sem, sem(g, 'd', h), to_y))
        elif source == 'y':
            pl.when((c == 0) | by_x)(lambda: send(piece, piece, spread_sem, sem(g, 'd', h), to_x))
        send(piece, piece, spread_sem, sem(g, 'core', h), to_core)

    groups = {'q': None, 'a': g_a, 'b': g_b, 'c': g_c}

    @scoped
    def ev(name, sources, *halves):
        for h in halves or (0, 1):
            for source in sources:
                pass_on(groups[name], source, h, name == 'q')

    @scoped
    def whole(name):
        if name == 'q':
            arrived(wq.at[1, pl.ds(0, 4 * q_rows), :], sem(None, 'core', 0))
        else:
            arrived(wo.at[pl.ds(0, 4 * o_rows), :], sem(groups[name], 'core', 0))

    loads[5].start()

    with jax.named_scope('load_wait'):
        for i in (0, 6, 7):
            loads[i].wait()
    gain = gain_ref[...].astype(F32)
    lnb = lnb_ref[...].astype(F32)
    ln_rows = min(64, tok)

    def ln_step(i, carry):
        rows = pl.ds(pl.multiple_of(i * ln_rows, ln_rows), ln_rows)
        x = hid[rows, :].astype(F32)
        cen = x - jnp.mean(x, axis=-1, keepdims=True)
        var = jnp.mean(cen * cen, axis=-1, keepdims=True)
        normed[rows, :] = (cen * lax.rsqrt(var + LN_EPS) * gain + lnb).astype(BF16)
        return carry

    with jax.named_scope('ln'):
        lax.fori_loop(0, tok // ln_rows, ln_step, 0)

    loads[1].wait()
    loads[8].wait()
    kv_new = (jnp.dot(normed[...], wkv[...], preferred_element_type=F32) + bkv_ref[...].astype(F32)).astype(BF16)
    kv[cp, 0] = kv_new[:, :HEAD_DIM]
    kv[cp, 1] = kv_new[:, HEAD_DIM:]
    k_ref[...] = kv_new[:, :HEAD_DIM]
    v_ref[...] = kv_new[:, HEAD_DIM:]

    @scoped
    def project_q(which, bias):
        qf = jnp.dot(normed[...], wq[which], preferred_element_type=F32) + bias[...].astype(F32)
        for r in range(4):
            for h in range(heads):
                q_s[which * 4 + r, h * tile:(h + 1) * tile, :] = qf[r * tile:(r + 1) * tile, h * HEAD_DIM:(h + 1) * HEAD_DIM].astype(BF16)

    loads[2].wait()
    loads[3].wait()
    for i in (0, 1):
        pl.when(y == 0)(lambda: send(kv.at[cp, i], kv.at[cp, i], kv_sem, kv_recv.at[cp, i], to_y))
    for i in (0, 1):
        pl.when(c == 0)(lambda: send(kv.at[cp, i], kv.at[cp, i], kv_sem, kv_recv.at[cp, i], to_core))
    project_q(0, bq_own)
    loads[4].wait()
    for r in range(4):
        row = jnp.broadcast_to(seg[cp, :, r * tile:(r + 1) * tile], (tile, tile))
        segcol[r] = row.T

    g_1, g_2 = 2 - z // 2, 3 - 3 * (z // 2)
    tile_rows = lambda r: pl.ds(pl.multiple_of(r * tile, tile), tile)
    every = pl.ds(0, tok)

    def scores(q, k_blk, mask):
        keys = k_blk.shape[0]
        s = lax.dot_general(q, k_blk, (((1,), (1,)), ((), ())), preferred_element_type=F32) * SCORE_SCALE
        return jnp.where(mask[None], s.reshape(heads, tile, keys), -jnp.inf).reshape(heads * tile, keys)

    @scoped
    def attend_own(t, carry):
        r = t % 4

        def step(keys):
            k_pos = lax.broadcasted_iota(jnp.int32, (tile, keys), 1)
            q_pos = lax.broadcasted_iota(jnp.int32, (tile, keys), 0) + r * tile
            s = scores(q_s[t], kv[cp, 0, :keys, :], (seg[cp, :, :keys] == segcol[r][:, :1]) & (k_pos <= q_pos))
            m_new = jnp.max(s, axis=-1, keepdims=True)
            p = jnp.exp2(s - m_new)
            m_s[r] = jnp.broadcast_to(m_new, m_s.shape[1:])
            l_s[r] = jnp.broadcast_to(jnp.sum(p, axis=-1, keepdims=True), l_s.shape[1:])
            acc_s[r] = jnp.dot(p.astype(BF16), kv[cp, 1, :keys, :], preferred_element_type=F32)

        pl.when(r < 2)(lambda: step(tok // 2))
        pl.when(r >= 2)(lambda: step(tok))
        return carry

    def attend_block(t, j):
        r = t % 4
        s = scores(q_s[t], kv[j, 0], seg[j] == segcol[r][:, :1])
        m_prev = m_s[r]
        m_new = jnp.maximum(m_prev, jnp.max(s, axis=-1, keepdims=True))
        p = jnp.exp2(s - m_new[:, :1])
        alpha = jnp.exp2(m_prev - m_new)
        m_s[r] = m_new
        l_s[r] = l_s[r] * alpha + jnp.sum(p, axis=-1, keepdims=True)
        acc_s[r] = acc_s[r] * alpha + jnp.dot(p.astype(BF16), kv[j, 1], preferred_element_type=F32)

    def attend_end(t, g):
        r = t % 4
        for h in range(heads):
            at = slice(h * tile, (h + 1) * tile)
            o_all[g, tile_rows(r), h * HEAD_DIM:(h + 1) * HEAD_DIM] = (acc_s[r, at, :] / l_s[r, at, :]).astype(BF16)

    def send_heads(t, g):
        o_tile = o_all.at[g, tile_rows(t % 4), :]
        pl.when(middle)(lambda: send(o_tile, o_tile, line_sem, o_recv.at[t], {'tp': 3 - z}))

    @scoped
    def heads_event(u):
        o_tile = o_all.at[g_1 if u < 4 else g_2, tile_rows(u % 4), :]
        arrived(o_tile, o_recv.at[u])
        for to, cond in ((0, z == 1), (3, z == 2)):
            pl.when(cond)(lambda: send(o_tile, o_tile, line_sem, o_recv.at[u], {'tp': to}))

    def heads_here(*tiles):
        on(middle, *((heads_event, u) for u in tiles))

    def on(cond, *todo):
        @pl.when(cond)
        def _():
            for what, *about in todo:
                what(*about)

    n_col = min(512, d_model)

    def project(g, rows, use):
        def cols(n, carry):
            at = pl.ds(pl.multiple_of(n * n_col, n_col), n_col)
            use(rows, at, jnp.dot(o_all[g, rows, :], wo[pl.ds(pl.multiple_of(g * width, width), width), at],
                                  preferred_element_type=F32).astype(BF16))
            return carry

        lax.fori_loop(0, d_model // n_col, cols, 0)

    @scoped
    def project_o(g):
        def keep(rows, at, fresh):
            part[g % 2, rows, at] = fresh

        project(g, every, keep)

    @scoped
    def project_third(g):
        def add(rows, at, fresh):
            pair_sum = part[(3 - g) % 2, rows, at].astype(F32) + fresh.astype(F32)
            run_s[rows, at] = hid[rows, at].astype(F32) + bo_ref[at].astype(F32) + pair_sum

        project(g, every, add)

    @scoped
    def project_last(g, rows):
        def add(rows, at, fresh):
            y_ref[rows, at] = (run_s[rows, at] + (part[(3 - g) % 2, rows, at].astype(F32) + fresh.astype(F32))).astype(BF16)

        project(g, rows, add)

    @scoped
    def kv_pass(i):
        @pl.when(y == 1)
        def _():
            arrived(kv.at[c, i], kv_recv.at[c, i])
            send(kv.at[c, i], kv.at[c, i], kv_sem, kv_recv.at[c, i], to_core)

    def own_block(t, carry):
        attend_own(t, carry)
        on(t == 0, (ev, 'q', 'zs', 0))
        on(t == 3, (kv_pass, 0))
        return carry

    lax.fori_loop(0, 4, own_block, 0)

    @pl.when(c == 1)
    def _():
        arrived(seg.at[cp - 1], seg_recv.at[cp - 1])
        for i in (0, 1):
            arrived(kv.at[cp - 1, i], kv_recv.at[cp - 1, i])

    def first_block(t, carry):
        pl.when(c == 1)(lambda: attend_block(t, cp - 1))
        on(t == 0, (ev, 'q', 'zs', 1))
        on(t == 1, (kv_pass, 1))
        on((t == 2) & middle, (ev, 'a', 'z', 0))
        on((t == 3) & middle, (ev, 'a', 'z', 1))
        on(t == 3, (ev, 'q', 'x', 0))
        on((t == 3) & middle, (ev, 'a', 's', 0))
        return carry

    lax.fori_loop(0, 4, first_block, 0)
    pl.when(y == 1)(lambda: arrived(seg.at[c], seg_recv.at[c]))

    def second_block(t, carry):
        pl.when(y == 1)(lambda: attend_block(t, c))
        on(t == 1, (ev, 'q', 'y', 0))
        on((t == 2) & middle, (ev, 'b', 'z', 0))
        on((t == 2) & edge, (ev, 'a', 'zs', 0))
        on(t == 3, (ev, 'q', 'x', 1))
        return carry

    lax.fori_loop(0, 4, second_block, 0)

    @pl.when(y == 1)
    def _():
        arrived(seg.at[1 - c], seg_recv.at[1 - c])
        for i in (0, 1):
            arrived(kv.at[1 - c, i], kv_recv.at[1 - c, i])

    def third_block(t, carry):
        pl.when(y == 1)(lambda: attend_block(t, 1 - c))
        attend_end(t, z)
        on((t == 0) & middle, (ev, 'b', 'z', 1))
        send_heads(t, z)
        on(t == 1, (ev, 'q', 'y', 1))
        on((t == 1) & middle, (ev, 'a', 's', 1))
        on((t == 2) & middle, (ev, 'b', 's', 0))
        on((t == 2) & edge, (ev, 'a', 'zs', 1))
        return carry

    lax.fori_loop(0, 4, third_block, 0)
    on(edge, (ev, 'b', 'zs', 0))
    on(middle, (ev, 'b', 's', 1), (ev, 'c', 'z', 0))
    ev('q', 'd', 0)
    loads[5].wait()
    project_o(z)
    ev('a', 'xy', 0)
    on(edge, (ev, 'b', 'zs', 1))
    ev('q', 'd', 1)
    on(middle, (ev, 'c', 'z', 1))
    whole('q')
    arrived(bq_pair, bq_recv)
    project_q(1, bq_pair)
    on(middle, (ev, 'c', 's', 0))
    ev('a', 'xy', 1)
    heads_here(0)
    on(edge, (ev, 'c', 'zs', 0))

    def pair_heads(t, carry):
        attend_own(t, carry)
        on((t == 4) & middle, (ev, 'c', 's', 1), (heads_event, 1))
        on((t == 5) & (y == 1), (ev, 'b', 'xy', 0))
        on((t == 6) & (y == 1), (ev, 'b', 'xy', 1))
        on((t == 6) & (y == 1) & middle, (heads_event, 4))
        on((t == 7) & (y == 1) & middle, (heads_event, 5))

        def block(j, inner):
            attend_block(t, j)
            return inner

        lax.fori_loop(0, cp, block, 0)
        attend_end(t, pair)
        send_heads(t, pair)
        on((t == 4) & edge, (ev, 'c', 'zs', 1))
        on((t == 4) & (y == 1) & middle, (heads_event, 2))
        on((t == 4) & (y == 1), (ev, 'a', 'd', 0))
        on((t == 5) & (y == 1) & middle, (heads_event, 3))
        on((t == 6) & (y == 1), (ev, 'a', 'd', 1), (ev, 'c', 'xy', 0))
        on((t == 7) & (y == 1), (ev, 'c', 'xy', 1))
        return carry

    lax.fori_loop(4, 8, pair_heads, 0)

    @pl.when(y == 0)
    def _():
        heads_here(2, 3)
        ev('b', 'xy', 0)
        ev('a', 'd', 0)
        heads_here(4)
        ev('b', 'xy', 1)
        heads_here(5)
        ev('a', 'd', 1)
        ev('c', 'xy', 0)
        ev('c', 'xy', 1)

    heads_here(6)
    ev('b', 'd')
    whole('a')
    loads[9].wait()
    on(edge, (project_o, pair))
    on(middle, (project_third, g_1))
    heads_here(7)
    whole('b')
    ev('c', 'd', 0)
    on(edge, *((heads_event, u) for u in range(4)))
    on(edge, (project_third, g_1))
    on(middle, (project_o, pair))
    ev('c', 'd', 1)
    whole('c')

    pl.when(middle)(lambda: project_last(g_2, every))

    def tile_event(r):
        arrived(o_all.at[g_2, tile_rows(r), :], o_recv.at[4 + r])

    def last(r, carry):
        tile_event(r)
        project_last(g_2, tile_rows(r))
        return carry

    @pl.when(edge)
    def _():
        tile_event(0)
        tile_event(1)
        project_last(g_2, pl.ds(0, 2 * tile))
        lax.fori_loop(2, 4, last, 0)

    with jax.named_scope('drain'):
        unit = o_rows // 2

        def sent(count, sems):
            arrived(wo.at[pl.ds(0, count * unit), :], sems)

        sent(58, spread_sem)
        pl.when(edge)(lambda: sent(2, line_sem))
        pl.when(middle)(lambda: sent(26, line_sem))
        for j in (0, 1):
            pl.when(c == j)(lambda: arrived(kv.at[pl.ds(0, 2 - j)], kv_sem))
        arrived(bq_pair, small_sem.at[0])
        for step in (1, 2, 3):
            pl.when(cp + step < 4)(lambda: arrived(seg.at[cp], small_sem.at[step]))


def write_out(y_in, k_in, v_in, y_out, k_out, v_out, sems):
    copies = [pltpu.make_async_copy(a, b, sems.at[i]) for i, (a, b) in enumerate(((y_in, y_out), (k_in, k_out), (v_in, v_out)))]
    for copy in copies:
        copy.start()
    for copy in copies:
        copy.wait()


def solution(mesh):
    def local_block(hidden, seg_ids, w_q, b_q, w_kv, b_kv, w_o, b_o, ln_gain, ln_bias):
        tok, d_model = hidden.shape
        width = w_q.shape[1]
        heads = width // HEAD_DIM
        tile = tok // 4
        hbm = pl.BlockSpec(memory_space=pltpu.HBM)
        vmem = pl.BlockSpec(memory_space=pltpu.VMEM)
        dma = pltpu.SemaphoreType.DMA
        far = lambda a: pltpu.with_memory_space_constraint(a, pltpu.HBM)
        outs = pl.pallas_call(
            kernel,
            out_shape=(jax.ShapeDtypeStruct((tok, d_model), BF16), jax.ShapeDtypeStruct((tok, HEAD_DIM), BF16),
                       jax.ShapeDtypeStruct((tok, HEAD_DIM), BF16)),
            in_specs=[hbm] * 10,
            out_specs=(vmem, vmem, vmem),
            scratch_shapes=[
                pltpu.VMEM((tok, d_model), BF16),
                pltpu.VMEM((tok, d_model), BF16),
                pltpu.VMEM((d_model, 2 * HEAD_DIM), BF16),
                pltpu.VMEM((2, d_model, width), BF16),
                pltpu.VMEM((4 * width, d_model), BF16),
                pltpu.VMEM((width,), BF16),
                pltpu.VMEM((width,), BF16),
                pltpu.VMEM((2 * HEAD_DIM,), BF16),
                pltpu.VMEM((d_model,), BF16),
                pltpu.VMEM((d_model,), BF16),
                pltpu.VMEM((d_model,), BF16),
                pltpu.VMEM((4, 1, tok), jnp.int32),
                pltpu.VMEM((4, tile, tile), jnp.int32),
                pltpu.VMEM((4, 2, tok, HEAD_DIM), BF16),
                pltpu.VMEM((8, heads * tile, HEAD_DIM), BF16),
                pltpu.VMEM((4, tok, width), BF16),
                pltpu.VMEM((2, tok, d_model), BF16),
                pltpu.VMEM((tok, d_model), F32),
                pltpu.VMEM((4, heads * tile, HEAD_DIM), F32),
                pltpu.VMEM((4, heads * tile, HEAD_DIM), F32),
                pltpu.VMEM((4, heads * tile, HEAD_DIM), F32),
                dma((10,)), dma(()), dma(()), dma(()), dma((4,)), dma(()), dma((4,)), dma((4, 2)), dma((9,)), dma((4, 9)), dma((8,)),
            ],
            compiler_params=pltpu.CompilerParams(collective_id=0, has_side_effects=True, vmem_limit_bytes=48 * 2 ** 20),
            name='block',
        )(far(hidden), far(seg_ids.reshape(1, -1)), far(w_q), far(b_q), far(w_kv), far(b_kv), far(w_o), far(b_o), far(ln_gain), far(ln_bias))
        near = lambda a: pltpu.with_memory_space_constraint(a, pltpu.VMEM)
        return pl.pallas_call(
            write_out,
            out_shape=tuple(jax.ShapeDtypeStruct(a.shape, a.dtype) for a in outs),
            in_specs=[vmem] * 3,
            out_specs=(pl.BlockSpec(memory_space=pl.ANY),) * 3,
            scratch_shapes=[dma((3,))],
            name='write',
        )(*map(near, outs))

    row_spec = P(('dp', 'cp'), None)
    tok_spec = P(('dp', 'cp'))
    return jax.shard_map(local_block, mesh=mesh,
                         in_specs=(row_spec, tok_spec, P(None, 'tp'), P('tp'), P(None, None), P(None), P('tp', None), P(None), P(None), P(None)),
                         out_specs=(row_spec, row_spec, row_spec), check_vma=False)
```

profile of v0, /device:TPU:0, one launch (start us, length us, event | category | flops | bytes accessed | tf_op | source)
XLA Modules:
  0.0 56.1 jit_solution(2230692925745095429)
XLA Ops:
  0.6 54.0 %block.1 = (bf16[512,2048]{1,0:T(8,128)(2,1)S(1)}, bf16[512,128]{1,0:T(8,128)(2,1)S(1)}, bf16[512,128]{1,0:T(8,128)(2,1)S(1)}) custom-call(bf16[512,2048]{1,0:T(8,128)(2,1)} %hid_hbm.1, s32[1,512]{1,0:T(1,128)} %bitcast.1, bf16[2048,512]{1,0:T(8,128)(2,1)} %wq_hbm.1, bf16[512]{0:T(512)(128)(2,1)} %bq_hbm.1, bf16[2048,256]{1,0:T(8,128)(2,1)} %wkv_hbm.1, ...), custom_call_target="tpu_custom_call" | custom-call | tf_op jit(solution)/shard_map/block/pallas_call | solution.py:471
  54.7 1.4 %write.1 = (bf16[512,2048]{1,0:T(8,128)(2,1)}, bf16[512,128]{1,0:T(8,128)(2,1)}, bf16[512,128]{1,0:T(8,128)(2,1)}) custom-call(bf16[512,2048]{1,0:T(8,128)(2,1)S(1)} %get-tuple-element.6.y_in, bf16[512,128]{1,0:T(8,128)(2,1)S(1)} %get-tuple-element.7.k_in, bf16[512,128]{1,0:T(8,128)(2,1)S(1)} %get-tuple-element.8.v_in), custom_call_target="tpu_custom_call" | custom-call | tf_op jit(solution)/shard_map/write/pallas_call | solution.py:505
where the time goes:
time: 56.9 us; the launch traced here: 56.1 us
  Pallas kernels  55.5 us (98%)
  between operations  0.64 us (1%)
    pallas_call x1, Pallas kernels, local_block(): pl.pallas_call(kernel, out_shape=(jax.ShapeDtypeStruct((tok, d_model), BF...  54 us
    pallas_call x1, Pallas kernels, local_block(): pl.pallas_call(write_out, out_shape=tuple((jax.ShapeDtypeStruct(a.shape,...  1.42 us

commit v1 on v0

--- a/solution.py
+++ b/solution.py
@@ -402,19 +402,20 @@
         ev('c', 'xy', 0)
         ev('c', 'xy', 1)
 
-    heads_here(6)
     ev('b', 'd')
     whole('a')
     loads[9].wait()
     on(edge, (project_o, pair))
+    heads_here(6)
     on(middle, (project_third, g_1))
     heads_here(7)
     whole('b')
     ev('c', 'd', 0)
     on(edge, *((heads_event, u) for u in range(4)))
+    on(middle, (ev, 'c', 'd', 1))
     on(edge, (project_third, g_1))
     on(middle, (project_o, pair))
-    ev('c', 'd', 1)
+    on(edge, (ev, 'c', 'd', 1))
     whole('c')
 
     pl.when(middle)(lambda: project_last(g_2, every))

time: 56.9 us -> 56.9 us (level)
  no operation moved by 1% of the time
where the time goes in v1:
time: 56.9 us; the launch traced here: 56.4 us
  Pallas kernels  55.7 us (98%)
  between operations  0.64 us (1%)
    pallas_call x1, Pallas kernels, local_block(): pl.pallas_call(kernel, out_shape=(jax.ShapeDtypeStruct((tok, d_model), BF...  54.3 us
    pallas_call x1, Pallas kernels, local_block(): pl.pallas_call(write_out, out_shape=tuple((jax.ShapeDtypeStruct(a.shape,...  1.42 us

profile of v1, /device:TPU:0, one launch (start us, length us, event | category | flops | bytes accessed | tf_op | source)
XLA Modules:
  0.0 56.4 jit_solution(8022514230917119864)
XLA Ops:
  0.6 54.3 %block.1 = (bf16[512,2048]{1,0:T(8,128)(2,1)S(1)}, bf16[512,128]{1,0:T(8,128)(2,1)S(1)}, bf16[512,128]{1,0:T(8,128)(2,1)S(1)}) custom-call(bf16[512,2048]{1,0:T(8,128)(2,1)} %hid_hbm.1, s32[1,512]{1,0:T(1,128)} %bitcast.1, bf16[2048,512]{1,0:T(8,128)(2,1)} %wq_hbm.1, bf16[512]{0:T(512)(128)(2,1)} %bq_hbm.1, bf16[2048,256]{1,0:T(8,128)(2,1)} %wkv_hbm.1, ...), custom_call_target="tpu_custom_call" | custom-call | tf_op jit(solution)/shard_map/block/pallas_call | solution.py:472
  54.9 1.4 %write.1 = (bf16[512,2048]{1,0:T(8,128)(2,1)}, bf16[512,128]{1,0:T(8,128)(2,1)}, bf16[512,128]{1,0:T(8,128)(2,1)}) custom-call(bf16[512,2048]{1,0:T(8,128)(2,1)S(1)} %get-tuple-element.6.y_in, bf16[512,128]{1,0:T(8,128)(2,1)S(1)} %get-tuple-element.7.k_in, bf16[512,128]{1,0:T(8,128)(2,1)S(1)} %get-tuple-element.8.v_in), custom_call_target="tpu_custom_call" | custom-call | tf_op jit(solution)/shard_map/write/pallas_call | solution.py:506
